TPU v7x, 32 devices: a whole 2x2x4 slice. The times are simulated.
32 devices in a mesh: tp: 8 (over z, core), fs: 4 (over y, x).
Axes of the slice: x: 2, y: 2, z: 4, core: 2. Of those that a mesh axis runs over, the one named last changes fastest.
Arguments:
- tokens: bfloat16 [128, 8192], P(('tp', 'fs')), may hold values from -6 to 6
- gate_weight: bfloat16 [8192, 29568], P('fs', 'tp'), may hold values from -0.0625 to 0.0625
- up_weight: bfloat16 [8192, 29568], P('fs', 'tp'), may hold values from -0.0625 to 0.0625
- down_weight: bfloat16 [29568, 8192], P('tp', 'fs'), may hold values from -0.046875 to 0.046875
Outputs:
- mixed: bfloat16 [128, 8192], P(None, ('fs', 'tp'))
All inputs are finite; a program needn't handle non-finite values.
Results may differ from a plain program's by a relative error of at most 0.0049.
Values may be sent and summed in bfloat16 or wider, within the bound.
A program may use at most 128 MiB of HBM per device.

v0:
```python
import jax
import jax.numpy as jnp
from jax import lax
from jax.sharding import PartitionSpec as P


def body(tokens, gate_weight, up_weight, down_weight):
    by_feature = lax.all_to_all(tokens, "fs", split_axis=1, concat_axis=0, tiled=True)
    feature_rows = lax.all_gather(by_feature, "tp", axis=0, tiled=True)
    gate_part = jnp.dot(feature_rows, gate_weight, preferred_element_type=jnp.float32)
    up_part = jnp.dot(feature_rows, up_weight, preferred_element_type=jnp.float32)
    gate, up = (
        lax.psum_scatter(gate_part, "fs", scatter_dimension=1, tiled=True),
        lax.psum_scatter(up_part, "fs", scatter_dimension=1, tiled=True),
    )
    hidden = (jax.nn.silu(gate) * up).astype(jnp.bfloat16)
    hidden_all = lax.all_gather(hidden, "fs", axis=1, tiled=True)
    partial_out = jnp.dot(hidden_all, down_weight, preferred_element_type=jnp.float32)
    summed = lax.psum_scatter(partial_out, "tp", scatter_dimension=1, tiled=True)
    return summed.astype(jnp.bfloat16)


def solution(mesh):
    return jax.shard_map(
        body,
        mesh=mesh,
        in_specs=(P(("tp", "fs"), None), P("fs", "tp"), P("fs", "tp"), P("tp", "fs")),
        out_specs=P(None, ("fs", "tp")),
        check_vma=False,
    )
```

profile of v0, /device:TPU:0, one launch (start us, length us, event | category | flops | bytes accessed | tf_op | source)
XLA Modules:
  0.0 184.2 jit_solution(5929641926974322343)
XLA Ops:
  6.5 0.0 reduce-scatter.6.cloned.1.call-start
  6.5 10.0 %all_to_all.19 = bf16[4,4,2048]{2,0,1:T(4,128)(2,1)S(1)} all-to-all(bf16[4,4,2048]{2,0,1:T(4,128)(2,1)} %bitcast.19), channel_id=1, replica_groups=mesh['tp'=8,'fs'=4] {'fs'}, dimensions={1} | all-to-all | bytes 131072 | tf_op jit(solution)/shard_map/all_to_all | solution.py:8
  16.6 0.0 copy-start
  16.6 15.1 %all_gather.6 = bf16[128,2048]{1,0:T(8,128)(2,1)S(1)} all-gather(bf16[16,2048]{1,0:T(8,128)(2,1)S(1)} %all_to_all.17), channel_id=1, replica_groups=mesh['tp'=8,'fs'=4] {'tp'}, dimensions={0}, use_global_device_ids=true | all-gather | bytes 589824 | tf_op jit(solution)/shard_map/all_gather | solution.py:9
  31.8 7.6 %fusion.5 = f32[128,3696]{0,1:T(8,128)S(1)} fusion(bf16[128,2048]{1,0:T(8,128)(2,1)S(1)} %all_gather.6, bf16[2048,3696]{0,1:T(8,128)(2,1)} %param.5), kind=kOutput, calls=%fused_computation.3 | convolution fusion | flops 1937768448 | bytes 17555456 | tf_op jit(solution)/shard_map/dot_general | solution.py:10
  39.3 0.0 copy-done
  39.3 0.0 copy-start.1
  39.4 5.6 %fusion.6 = f32[128,3696]{0,1:T(8,128)} fusion(bf16[128,2048]{1,0:T(8,128)(2,1)S(1)} %all_gather.6, bf16[2048,3696]{0,1:T(8,128)(2,1)S(1)} %copy-done), kind=kOutput, calls=%fused_computation.4 | convolution fusion | flops 1937768448 | bytes 17555456 | tf_op jit(solution)/shard_map/dot_general | solution.py:11
  44.9 67.6 %fusion.4 = (f32[128,928]{0,1:T(8,128)S(1)}, f32[128,928]{0,1:T(8,128)S(1)}) fusion(f32[128,3696]{0,1:T(8,128)} %fusion.6, f32[128,3696]{0,1:T(8,128)S(1)} %fusion.5), kind=kCustom, calls=%all-reduce-scatter.2 | all-reduce-scatter fusion | flops 950273 | bytes 4735488
  112.6 1.7 collective-permute-start
  114.3 4.3 %collective-permute-start.1 = (f32[128,12]{0,1:T(8,128)S(1)}, f32[128,12]{0,1:T(8,128)S(1)}, u32[]{:S(2)}, u32[]{:S(2)}) collective-permute-start(f32[128,12]{0,1:T(8,128)S(1)} %slice.1), channel_id=1, source_target_pairs={{0,1},{1,2},{2,3},{4,5},{5,6},{6,7},{8,9},{9,10},{10,11},{12,13},{... | collective-permute-start | bytes 18440
  118.6 0.0 copy-done.1
  118.6 0.6 dynamic-slice.6
  119.9 0.0 collective-permute-done
  119.9 1.1 concatenate
  121.0 0.0 collective-permute-done.1
  121.0 1.1 concatenate.1
  122.1 0.2 fusion.3
  122.3 12.0 %all-gather = bf16[4,924,128]{2,1,0:T(8,128)(2,1)S(1)} all-gather(bf16[1,924,128]{2,1,0:T(8,128)(2,1)S(1)} %fusion.3), channel_id=1, replica_groups=mesh['tp'=8,'fs'=4] {'fs'}, dimensions={0}, use_global_device_ids=true | all-gather | bytes 1182720 | tf_op jit(solution)/shard_map/all_gather | solution.py:17
  134.3 0.2 reshape.4
  134.5 8.5 %fusion.7 = f32[128,2048]{1,0:T(8,128)} fusion(bf16[3696,128]{1,0:T(8,128)(2,1)S(1)} %reshape.4, bf16[3696,2048]{1,0:T(8,128)(2,1)} %param.7), kind=kOutput, calls=%fused_computation.5 | convolution fusion | flops 1937768448 | bytes 17133568 | tf_op jit(solution)/shard_map/dot_general | solution.py:18
  143.0 0.0 reduce-scatter.6.cloned.1.call-update
  143.0 32.8 %reduce-scatter.6.cloned.1.call-done = f32[128,256]{1,0:T(8,128)} async-done(((f32[128,2048]{1,0:T(8,128)}), f32[128,256]{1,0:T(8,128)}) %reduce-scatter.6.cloned.1.call-update) | async-done | bytes 131088 | tf_op jit(solution)/shard_map/reduce_scatter | solution.py:19
  175.8 1.5 convert_element_type.7
  (3 shorter events, 0.0 us)
Async XLA Ops:
  6.5 169.3 %reduce-scatter.6.cloned.1.call-start = ((), (), s32[]{:S(2)}) async-start(), calls=%async_computation.2 | async-start | bytes 1179648 | tf_op jit(solution)/shard_map/reduce_scatter | solution.py:19
  16.6 22.7 %copy-start = (bf16[2048,3696]{0,1:T(8,128)(2,1)S(1)}, bf16[2048,3696]{0,1:T(8,128)(2,1)}, u32[]{:S(2)}) copy-start(bf16[2048,3696]{0,1:T(8,128)(2,1)} %param.6) | copy-start | bytes 45416452
  39.3 79.3 %copy-start.1 = (u32[32]{0:T(128)S(1)}, u32[32]{0:T(128)}, u32[]{:S(2)}) copy-start(u32[32]{0:T(128)} %constant.6) | copy-start | bytes 388
  112.6 7.3 %collective-permute-start = (f32[128,12]{0,1:T(8,128)S(1)}, f32[128,12]{0,1:T(8,128)S(1)}, u32[]{:S(2)}, u32[]{:S(2)}) collective-permute-start(f32[128,12]{0,1:T(8,128)S(1)} %slice), channel_id=1, source_target_pairs={{0,1},{1,2},{2,3},{4,5},{5,6},{6,7},{8,9},{9,10},{10,11},{12,13},{... | collective-permute-start | bytes 18440
  114.3 6.7 %collective-permute-start.1 = (f32[128,12]{0,1:T(8,128)S(1)}, f32[128,12]{0,1:T(8,128)S(1)}, u32[]{:S(2)}, u32[]{:S(2)}) collective-permute-start(f32[128,12]{0,1:T(8,128)S(1)} %slice.1), channel_id=1, source_target_pairs={{0,1},{1,2},{2,3},{4,5},{5,6},{6,7},{8,9},{9,10},{10,11},{12,13},{... | collective-permute-start | bytes 18440
Sparse Core Ops, SparseCore 0:
  143.1 32.6 reduce-scatter.5
where the time goes:
time: 185 us; the launch traced here: 184 us
  blocking collectives  105 us (57%)
  waiting for transfers between devices  32.9 us (18%)
  matrix products  21.6 us (12%)
  between operations  14.2 us (8%)
  starting transfers between devices  6.01 us (3%)
  local copies, waits for them, and re-layouts  3.02 us (2%)
    unnamed x1, blocking collectives  67.6 us
    reduce_scatter x1, waiting for transfers between devices, body(): lax.psum_scatter(partial_out, 'tp', scatter_dimension=1, tiled=True)  32.8 us
    all_gather x1, blocking collectives, body(): feature_rows = lax.all_gather(by_feature, 'tp', axis=0, tiled=True)  15.1 us
    all_gather x1, blocking collectives, body(): hidden_all = lax.all_gather(hidden, 'fs', axis=1, tiled=True)  12 us
    all_to_all x1, blocking collectives, body(): lax.all_to_all(tokens, 'fs', split_axis=1, concat_axis=0, tiled=True)  10 us
    dot_general x1, matrix products, body(): jnp.dot(hidden_all, down_weight, preferred_element_type=jnp.float32)  8.5 us
    dot_general x1, matrix products, body(): jnp.dot(feature_rows, gate_weight, preferred_element_type=jnp.float32)  7.58 us
    unnamed x2, starting transfers between devices  6.01 us
  transfers between devices with their start and end apart: 3, of which 1 were waited for; matrix products, arithmetic and copies ran while one was open for 1% of the time, Pallas kernels for 0%

commit v1 on v0

--- a/solution.py
+++ b/solution.py
@@ -2,6 +2,19 @@
 import jax.numpy as jnp
 from jax import lax
 from jax.sharding import PartitionSpec as P
+
+
+def _cover_pages(my_data, link_axis):
+    width = jax.lax.axis_size(link_axis)
+    current_value = [None] * width
+    lanes = list(map(lambda w: (w, (w + 1) % width), range(width)))
+    current_value[width - 1] = my_data
+    for dev_j in range(width - 2, -1, -1):
+        current_value[dev_j] = jax.lax.ppermute(current_value[dev_j + 1], link_axis, lanes)
+    extra = jnp.concatenate(current_value, 1)
+    base_arr = (jax.lax.axis_index(link_axis) + 1) * my_data.shape[1]
+    s_next = jnp.roll(extra, base_arr, 1)
+    return s_next
 
 
 def body(tokens, gate_weight, up_weight, down_weight):
@@ -14,7 +27,7 @@
         lax.psum_scatter(up_part, "fs", scatter_dimension=1, tiled=True),
     )
     hidden = (jax.nn.silu(gate) * up).astype(jnp.bfloat16)
-    hidden_all = lax.all_gather(hidden, "fs", axis=1, tiled=True)
+    hidden_all = _cover_pages(hidden, "fs")
     partial_out = jnp.dot(hidden_all, down_weight, preferred_element_type=jnp.float32)
     summed = lax.psum_scatter(partial_out, "tp", scatter_dimension=1, tiled=True)
     return summed.astype(jnp.bfloat16)

time: 185 us -> 200 us (1.081)
  waiting for transfers between devices: 32.9 us -> 53.2 us
  blocking collectives: 105 us -> 92.8 us
  local copies, waits for them, and re-layouts: 3.02 us -> 8.72 us
    ppermute x0 -> x3, waiting for transfers between devices: none -> 20.3 us  [_cover_pages(): jax.lax.ppermute(current_value[dev_j + 1], link_axis, lanes)]
    all_gather x1 -> x0, blocking collectives: 12 us -> none  [body(): hidden_all = lax.all_gather(hidden, 'fs', axis=1, tiled=True)]
    concatenate x0 -> x1, local copies, waits for them, and re-layouts: none -> 4 us  [_cover_pages(): s_next = jnp.roll(extra, base_arr, 1)]
    unnamed x10 -> x9, local copies, waits for them, and re-layouts: 3 us -> 4.7 us
  transfers between devices with their start and end apart: 3 -> 6, of which waited for: 1 -> 4; matrix products, arithmetic and copies ran while one was open for 1% -> 1% of each run, Pallas kernels for 0% -> 0%
where the time goes in v1:
time: 200 us
  blocking collectives  92.8 us (46%)
  waiting for transfers between devices  53.2 us (27%)
  matrix products  21.8 us (11%)
  between operations  14.1 us (7%)
  local copies, waits for them, and re-layouts  8.72 us (4%)
  starting transfers between devices  7.26 us (4%)
    unnamed x1, blocking collectives  67.8 us
    reduce_scatter x1, waiting for transfers between devices, body(): lax.psum_scatter(partial_out, 'tp', scatter_dimension=1, tiled=True)  32.8 us
    ppermute x3, waiting for transfers between devices, _cover_pages(): jax.lax.ppermute(current_value[dev_j + 1], link_axis, lanes)  20.3 us
    all_gather x1, blocking collectives, body(): feature_rows = lax.all_gather(by_feature, 'tp', axis=0, tiled=True)  15 us
    all_to_all x1, blocking collectives, body(): lax.all_to_all(tokens, 'fs', split_axis=1, concat_axis=0, tiled=True)  10 us
    dot_general x1, matrix products, body(): jnp.dot(hidden_all, down_weight, preferred_element_type=jnp.float32)  8.56 us
    dot_general x1, matrix products, body(): jnp.dot(feature_rows, gate_weight, preferred_element_type=jnp.float32)  7.73 us
    unnamed x2, starting transfers between devices  6.01 us
  transfers between devices with their start and end apart: 6, of which 4 were waited for; matrix products, arithmetic and copies ran while one was open for 1% of the time, Pallas kernels for 0%

profile of v1, /device:TPU:0, one launch (start us, length us, event | category | flops | bytes accessed | tf_op | source)
XLA Modules:
  0.0 199.7 jit_solution(17973246119653587589)
XLA Ops:
  6.5 0.0 reduce-scatter.6.cloned.1.call-start
  6.5 10.0 %all_to_all.19 = bf16[4,4,2048]{2,0,1:T(4,128)(2,1)S(1)} all-to-all(bf16[4,4,2048]{2,0,1:T(4,128)(2,1)} %bitcast.14), channel_id=1, replica_groups=mesh['tp'=8,'fs'=4] {'fs'}, dimensions={1} | all-to-all | bytes 131072 | tf_op jit(solution)/shard_map/all_to_all | solution.py:21
  16.6 15.0 %all_gather.3 = bf16[128,2048]{1,0:T(8,128)(2,1)S(1)} all-gather(bf16[16,2048]{1,0:T(8,128)(2,1)S(1)} %all_to_all.17), channel_id=1, replica_groups=mesh['tp'=8,'fs'=4] {'tp'}, dimensions={0}, use_global_device_ids=true | all-gather | bytes 589824 | tf_op jit(solution)/shard_map/all_gather | solution.py:22
  31.6 0.0 copy-start
  31.6 7.7 %fusion.7 = f32[128,3696]{0,1:T(8,128)S(1)} fusion(bf16[128,2048]{1,0:T(8,128)(2,1)S(1)} %all_gather.3, bf16[2048,3696]{0,1:T(8,128)(2,1)} %param.5), kind=kOutput, calls=%fused_computation.5 | convolution fusion | flops 1937768448 | bytes 17555456 | tf_op jit(solution)/shard_map/dot_general | solution.py:23
  39.3 1.9 copy-done
  41.2 5.6 %fusion.8 = f32[128,3696]{0,1:T(8,128)} fusion(bf16[128,2048]{1,0:T(8,128)(2,1)S(1)} %all_gather.3, bf16[2048,3696]{0,1:T(8,128)(2,1)S(1)} %copy-done), kind=kOutput, calls=%fused_computation.6 | convolution fusion | flops 1937768448 | bytes 17555456 | tf_op jit(solution)/shard_map/dot_general | solution.py:24
  46.8 0.0 copy-start.1
  46.8 67.8 %fusion.6 = (f32[128,928]{0,1:T(8,128)S(1)}, f32[128,928]{0,1:T(8,128)S(1)}) fusion(f32[128,3696]{0,1:T(8,128)} %fusion.8, f32[128,3696]{0,1:T(8,128)S(1)} %fusion.7), kind=kCustom, calls=%all-reduce-scatter.2 | all-reduce-scatter fusion | flops 950273 | bytes 4735488
  114.6 1.8 collective-permute-start.3
  116.3 4.3 %collective-permute-start.4 = (f32[128,12]{0,1:T(8,128)S(1)}, f32[128,12]{0,1:T(8,128)S(1)}, u32[]{:S(2)}, u32[]{:S(2)}) collective-permute-start(f32[128,12]{0,1:T(8,128)S(1)} %slice.1), channel_id=1, source_target_pairs={{0,1},{1,2},{2,3},{4,5},{5,6},{6,7},{8,9},{9,10},{10,11},{12,13},{... | collective-permute-start | bytes 18440
  120.6 0.0 copy-done.1
  120.6 0.6 dynamic-slice.6
  121.8 0.0 collective-permute-done.3
  121.9 1.1 concatenate.7
  123.0 0.0 collective-permute-done.4
  123.0 1.1 concatenate.8
  124.1 0.2 fusion.4
  124.3 1.2 collective-permute-start
  125.6 6.3 %collective-permute-done = bf16[128,924]{0,1:T(8,128)(2,1)S(1)} collective-permute-done((bf16[128,924]{0,1:T(8,128)(2,1)S(1)}, bf16[128,924]{0,1:T(8,128)(2,1)S(1)}, u32[]{:S(2)}, u32[]{:S(2)}) %collective-permute-start) | collective-permute-done | bytes 236576 | tf_op jit(solution)/shard_map/ppermute | solution.py:13
  131.9 0.0 collective-permute-start.1
  131.9 7.0 %collective-permute-done.1 = bf16[128,924]{0,1:T(8,128)(2,1)S(1)} collective-permute-done((bf16[128,924]{0,1:T(8,128)(2,1)S(1)}, bf16[128,924]{0,1:T(8,128)(2,1)S(1)}, u32[]{:S(2)}, u32[]{:S(2)}) %collective-permute-start.1) | collective-permute-done | bytes 236576 | tf_op jit(solution)/shard_map/ppermute | solution.py:13
  138.9 0.0 collective-permute-start.2
  138.9 7.0 %collective-permute-done.2 = bf16[128,924]{0,1:T(8,128)(2,1)S(1)} collective-permute-done((bf16[128,924]{0,1:T(8,128)(2,1)S(1)}, bf16[128,924]{0,1:T(8,128)(2,1)S(1)}, u32[]{:S(2)}, u32[]{:S(2)}) %collective-permute-start.2) | collective-permute-done | bytes 236576 | tf_op jit(solution)/shard_map/ppermute | solution.py:13
  145.9 4.0 %concatenate.6 = bf16[128,7392]{0,1:T(8,128)(2,1)S(1)} concatenate(bf16[128,924]{0,1:T(8,128)(2,1)S(1)} %collective-permute-done.2, bf16[128,924]{0,1:T(8,128)(2,1)S(1)} %collective-permute-done.1, bf16[128,924]{0,1:T(8,128)(2,1)S(1)} %collective-permute-done, bf16[128,924]{0,1:T(8,128)(2,1)S(1)} %fusion.4, bf16[128,924]{0,1:T(8,128)(2,1)S(1)} %collective-permute-done.2, ...), dimensions={1} | concatenate | bytes 3784704 | tf_op jit(solution)/shard_map/jit(_roll_dynamic)/concatenate | solution.py:16
  149.9 8.6 %fusion.2 = f32[128,2048]{1,0:T(8,128)} fusion(bf16[3696,2048]{1,0:T(8,128)(2,1)} %param.7, bf16[128,7392]{0,1:T(8,128)(2,1)S(1)} %concatenate.6, s32[]{:T(128)S(6)} %select_n.14), kind=kOutput, calls=%fused_computation | convolution fusion | flops 1937768448 | bytes 17133572 | tf_op jit(solution)/shard_map/dot_general | solution.py:31
  158.5 0.0 reduce-scatter.6.cloned.1.call-update
  158.5 32.8 %reduce-scatter.6.cloned.1.call-done = f32[128,256]{1,0:T(8,128)} async-done(((f32[128,2048]{1,0:T(8,128)}), f32[128,256]{1,0:T(8,128)}) %reduce-scatter.6.cloned.1.call-update) | async-done | bytes 131088 | tf_op jit(solution)/shard_map/reduce_scatter | solution.py:32
  191.3 1.5 convert_element_type.7
  (3 shorter events, 0.0 us)
Async XLA Ops:
  6.5 184.7 %reduce-scatter.6.cloned.1.call-start = ((), (), s32[]{:S(2)}) async-start(), calls=%async_computation.2 | async-start | bytes 1179648 | tf_op jit(solution)/shard_map/reduce_scatter | solution.py:32
  31.6 9.6 %copy-start = (bf16[2048,3696]{0,1:T(8,128)(2,1)S(1)}, bf16[2048,3696]{0,1:T(8,128)(2,1)}, u32[]{:S(2)}) copy-start(bf16[2048,3696]{0,1:T(8,128)(2,1)} %param.6) | copy-start | bytes 45416452
  46.8 73.8 %copy-start.1 = (u32[32]{0:T(128)S(1)}, u32[32]{0:T(128)}, u32[]{:S(2)}) copy-start(u32[32]{0:T(128)} %constant.33) | copy-start | bytes 388
  114.6 7.3 %collective-permute-start.3 = (f32[128,12]{0,1:T(8,128)S(1)}, f32[128,12]{0,1:T(8,128)S(1)}, u32[]{:S(2)}, u32[]{:S(2)}) collective-permute-start(f32[128,12]{0,1:T(8,128)S(1)} %slice), channel_id=1, source_target_pairs={{0,1},{1,2},{2,3},{4,5},{5,6},{6,7},{8,9},{9,10},{10,11},{12,13},{... | collective-permute-start | bytes 18440
  116.3 6.6 %collective-permute-start.4 = (f32[128,12]{0,1:T(8,128)S(1)}, f32[128,12]{0,1:T(8,128)S(1)}, u32[]{:S(2)}, u32[]{:S(2)}) collective-permute-start(f32[128,12]{0,1:T(8,128)S(1)} %slice.1), channel_id=1, source_target_pairs={{0,1},{1,2},{2,3},{4,5},{5,6},{6,7},{8,9},{9,10},{10,11},{12,13},{... | collective-permute-start | bytes 18440
  124.3 7.6 %collective-permute-start = (bf16[128,924]{0,1:T(8,128)(2,1)S(1)}, bf16[128,924]{0,1:T(8,128)(2,1)S(1)}, u32[]{:S(2)}, u32[]{:S(2)}) collective-permute-start(bf16[128,924]{0,1:T(8,128)(2,1)S(1)} %fusion.4), channel_id=1, source_target_pairs={{0,1},{1,2},{2,3},{3,0},{4,5},{5,6},{6,7},{7,4},{8,9},{9,10},{10,1... | collective-permute-start | bytes 709640 | tf_op jit(solution)/shard_map/ppermute | solution.py:13
  131.9 7.0 %collective-permute-start.1 = (bf16[128,924]{0,1:T(8,128)(2,1)S(1)}, bf16[128,924]{0,1:T(8,128)(2,1)S(1)}, u32[]{:S(2)}, u32[]{:S(2)}) collective-permute-start(bf16[128,924]{0,1:T(8,128)(2,1)S(1)} %collective-permute-done), channel_id=1, source_target_pairs={{0,1},{1,2},{2,3},{3,0},{4,5},{5,6},{6,7},{7,4},{8,9},{9,10},{10,1... | collective-permute-start | bytes 709640 | tf_op jit(solution)/shard_map/ppermute | solution.py:13
  138.9 7.0 %collective-permute-start.2 = (bf16[128,924]{0,1:T(8,128)(2,1)S(1)}, bf16[128,924]{0,1:T(8,128)(2,1)S(1)}, u32[]{:S(2)}, u32[]{:S(2)}) collective-permute-start(bf16[128,924]{0,1:T(8,128)(2,1)S(1)} %collective-permute-done.1), channel_id=1, source_target_pairs={{0,1},{1,2},{2,3},{3,0},{4,5},{5,6},{6,7},{7,4},{8,9},{9,10},{10,1... | collective-permute-start | bytes 709640 | tf_op jit(solution)/shard_map/ppermute | solution.py:13
Sparse Core Ops, SparseCore 0:
  158.6 32.6 reduce-scatter.5
